TPU v7x, 32 devices: a whole 2x2x4 slice. The times are simulated.
32 devices in a mesh: db: 8 (over z, y), sub: 4 (over x, core).
Axes of the slice: x: 2, y: 2, z: 4, core: 2. Of those that a mesh axis runs over, the one named last changes fastest.
Arguments:
- codes: int32 [8192, 64], P('db', 'sub'), may hold values from 0 to 255
- tables: bfloat16 [512, 64, 256], P('db', 'sub'), may hold values from 0.125 to 128, as said below
- limits: int32 [512], replicated, may hold values from 3008 to 3263
Outputs:
- hit_ids: int32 [512, 128], P(('db', 'sub'))
- hit_count: int32 [512], P(('db', 'sub'))
Inputs may be any that keep to these rules, and one draw needn't show every extreme that they name: `tables`: each value is a bfloat16 number of at least 1/8 and at most 128.
All inputs are finite; a program needn't handle non-finite values.
Results may differ from a plain program's by a relative error of at most 0.000001.
Values may be sent and summed in bfloat16 or wider, within the bound.
A program may use at most 128 MiB of HBM per device.

v0:
```python
import functools

import jax
import jax.numpy as jnp
from jax import lax
from jax.experimental import pallas as pl
from jax.experimental.pallas import tpu as pltpu
from jax.sharding import PartitionSpec as P

K = 256
SLOTS = 128
LANES = 128
COLS = 256
MESH = pl.DeviceIdType.MESH


def flip(index, other, size):
    both = 0
    bit = 1
    while bit < size:
        both = both + bit * (((index // bit) % 2) * ((other // bit) % 2))
        bit *= 2
    return index + other - 2 * both


def kernel(
    groups,
    codes_ref,
    tables_ref,
    limits_ref,
    ids_ref,
    count_ref,
    codes_all,
    part,
    recv1,
    send2,
    recv2,
    running,
    total,
    chosen,
    code_send,
    code_recv,
    send1_sem,
    recv1_sem,
    send2_sem,
    recv2_sem,
):
    db = lax.axis_index("db")
    sub = lax.axis_index("sub")
    low = sub % 2
    high = sub // 2
    near = sub + 1 - 2 * low
    far = sub + 2 - 4 * high
    width, rows = codes_ref.shape
    mine = ids_ref.shape[0]

    barrier = pltpu.get_barrier_semaphore()
    for step in range(1, groups):
        pl.semaphore_signal(
            barrier, inc=1, device_id={"db": flip(db, step, groups)}, device_id_type=MESH
        )
    pl.semaphore_signal(barrier, inc=1, device_id={"sub": near}, device_id_type=MESH)
    pl.semaphore_signal(barrier, inc=1, device_id={"sub": far}, device_id_type=MESH)
    pl.semaphore_wait(barrier, groups + 1)

    def code_copy(step):
        return pltpu.make_async_remote_copy(
            src_ref=codes_ref,
            dst_ref=codes_all.at[db],
            send_sem=code_send.at[step],
            recv_sem=code_recv.at[step],
            device_id={"db": flip(db, step, groups)},
            device_id_type=MESH,
        )

    def near_copy(source):
        return pltpu.make_async_remote_copy(
            src_ref=part.at[source, 1 - low],
            dst_ref=recv1.at[source],
            send_sem=send1_sem.at[source],
            recv_sem=recv1_sem.at[source],
            device_id={"sub": near},
            device_id_type=MESH,
        )

    def far_copy(source):
        return pltpu.make_async_remote_copy(
            src_ref=send2.at[source],
            dst_ref=recv2.at[source],
            send_sem=send2_sem.at[source],
            recv_sem=recv2_sem.at[source],
            device_id={"sub": far},
            device_id_type=MESH,
        )

    for step in range(1, groups):
        code_copy(step).start()
    codes_all[db] = codes_ref[...]

    centroid = lax.broadcasted_iota(jnp.int32, (K, LANES), 0).astype(jnp.float32)
    centroid = centroid.astype(jnp.bfloat16).reshape(K // 16, 16, LANES)
    centroid = jnp.concatenate([centroid] * (COLS // LANES), axis=2)

    def pass_on(step):
        source = flip(db, step, groups)
        near_copy(source).wait_recv()
        send2[source] = part[source, low, 1 - high] + recv1[source, 1 - high]
        far_copy(source).start()

    def score(step, carry):
        source = flip(db, step, groups)

        @pl.when(step > 0)
        def _():
            code_copy(step).wait_recv()

        def tile(j, carry):
            start = pl.multiple_of(j * COLS, COLS)
            local = codes_all[source, :, pl.ds(start, COLS)].astype(jnp.float32)
            acc = None
            for m in range(width):
                row = jnp.broadcast_to(local[m : m + 1, :], (16, COLS)).astype(jnp.bfloat16)
                hot = jnp.where(
                    centroid == row[None], jnp.bfloat16(1), jnp.bfloat16(0)
                ).reshape(K, COLS)
                term = jnp.dot(tables_ref[m], hot, preferred_element_type=jnp.float32)
                acc = term if acc is None else acc + term
            part[source, :, :, :, pl.ds(start, COLS)] = acc.reshape(2, 2, mine, COLS)
            return carry

        lax.fori_loop(0, rows // COLS, tile, 0, unroll=True)
        near_copy(source).start()

        @pl.when(step > 0)
        def _():
            pass_on(step - 1)

        return carry

    lax.fori_loop(0, groups, score, 0)
    pass_on(groups - 1)

    diagonal = lax.broadcasted_iota(jnp.int32, (mine, mine), 0) == lax.broadcasted_iota(
        jnp.int32, (mine, mine), 1
    )
    limit_row = jnp.broadcast_to(limits_ref[...].astype(jnp.float32), (mine, mine))
    limit = jnp.sum(jnp.where(diagonal, limit_row, 0.0), axis=1, keepdims=True)
    limit = jnp.broadcast_to(limit, (mine, LANES))
    blocks = rows // LANES
    upper_row = lax.broadcasted_iota(jnp.int32, (LANES, 2 * LANES), 0)
    upper_col = lax.broadcasted_iota(jnp.int32, (LANES, 2 * LANES), 1)
    upper = jnp.where(upper_row <= upper_col, 1.0, 0.0).astype(jnp.bfloat16)

    def match(step, carry):
        source = flip(db, step, groups)
        far_copy(source).wait_recv()
        flags = []
        for b in range(blocks):
            cut = pl.ds(b * LANES, LANES)
            distance = (
                part[source, low, high, :, cut]
                + recv1[source, high, :, cut]
                + recv2[source, :, cut]
            )
            flags.append(jnp.where(distance <= limit, 1.0, 0.0).astype(jnp.bfloat16))
        sums = jnp.dot(
            jnp.concatenate(flags, axis=0), upper, preferred_element_type=jnp.float32
        )
        here = pl.ds(pl.multiple_of(source * (blocks * mine), blocks * mine), blocks * mine)
        running[here, :] = sums[:, :LANES]
        total[here, :] = sums[:, LANES:]
        return carry

    lax.fori_loop(0, groups, match, 0)

    slot = lax.broadcasted_iota(jnp.int32, (mine, SLOTS), 1).astype(jnp.float32)

    def choose(b, carry):
        before, base, index, was = carry
        here = pl.ds(pl.multiple_of(b * mine, mine), mine)
        after = before + total[here, :]
        passed = jnp.where(after <= slot, 1.0, 0.0)
        chosen[here, :] = was - passed
        return after, jnp.where(after <= slot, after, base), index + passed, passed

    zero = jnp.zeros((mine, SLOTS), jnp.float32)
    found, base, index, _ = lax.fori_loop(
        0, groups * blocks, choose, (zero, zero, zero, zero + 1.0), unroll=8
    )
    rest = slot - base

    out = []
    for q in range(mine):
        every = pl.ds(q, groups * blocks, stride=mine)
        picked = lax.dot_general(
            running[every, :].astype(jnp.bfloat16),
            chosen[every, :].astype(jnp.bfloat16),
            (((0,), (0,)), ((), ())),
            preferred_element_type=jnp.float32,
        )
        below = jnp.where(picked <= rest[q : q + 1, :], 1.0, 0.0)
        out.append(jnp.sum(below, axis=0, keepdims=True))
    inside = jnp.concatenate(out, axis=0)
    ids_ref[...] = jnp.where(slot < found, index * LANES + inside, -1.0).astype(jnp.int32)
    count_ref[...] = jnp.sum(
        jnp.where(diagonal, found[:, :mine], 0.0), axis=0, keepdims=True
    ).astype(jnp.int32)

    def drain(step, carry):
        source = flip(db, step, groups)

        @pl.when(step > 0)
        def _():
            code_copy(step).wait_send()

        near_copy(source).wait_send()
        far_copy(source).wait_send()
        return carry

    lax.fori_loop(0, groups, drain, 0)


def per_device(groups, parts, codes, tables, limits):
    assert parts == 4 and groups & (groups - 1) == 0
    rows, width = codes.shape
    queries = tables.shape[0]
    mine = queries // parts
    db = lax.axis_index("db")
    sub = lax.axis_index("sub")
    codes_t = codes.T.astype(jnp.bfloat16)
    ordered = tables.reshape(2, 2, mine, width, K).transpose(3, 1, 0, 2, 4)
    ordered = ordered.reshape(width, queries, K)
    limit = lax.dynamic_slice_in_dim(limits, (db * parts + sub) * mine, mine)[None, :]
    blocks = groups * rows // LANES
    ids, counts = pl.pallas_call(
        functools.partial(kernel, groups),
        out_shape=(
            jax.ShapeDtypeStruct((mine, SLOTS), jnp.int32),
            jax.ShapeDtypeStruct((1, mine), jnp.int32),
        ),
        in_specs=[pl.BlockSpec(memory_space=pltpu.VMEM)] * 3,
        out_specs=[pl.BlockSpec(memory_space=pltpu.VMEM)] * 2,
        scratch_shapes=[
            pltpu.VMEM((groups, width, rows), jnp.bfloat16),
            pltpu.VMEM((groups, 2, 2, mine, rows), jnp.float32),
            pltpu.VMEM((groups, 2, mine, rows), jnp.float32),
            pltpu.VMEM((groups, mine, rows), jnp.float32),
            pltpu.VMEM((groups, mine, rows), jnp.float32),
            pltpu.VMEM((blocks * mine, LANES), jnp.float32),
            pltpu.VMEM((blocks * mine, LANES), jnp.float32),
            pltpu.VMEM((blocks * mine, LANES), jnp.float32),
            pltpu.SemaphoreType.DMA((groups,)),
            pltpu.SemaphoreType.DMA((groups,)),
            pltpu.SemaphoreType.DMA((groups,)),
            pltpu.SemaphoreType.DMA((groups,)),
            pltpu.SemaphoreType.DMA((groups,)),
            pltpu.SemaphoreType.DMA((groups,)),
        ],
        compiler_params=pltpu.CompilerParams(
            collective_id=0, has_side_effects=True, vmem_limit_bytes=60 * 1024 * 1024
        ),
        name="retrieve",
    )(codes_t, ordered, limit)
    return ids, counts[0]


def solution(mesh):
    placed = (P("db", "sub"), P("db", "sub", None), P())
    return jax.shard_map(
        functools.partial(per_device, mesh.shape["db"], mesh.shape["sub"]),
        mesh=mesh,
        in_specs=placed,
        out_specs=(P(("db", "sub"), None), P(("db", "sub"))),
        check_vma=False,
    )
```

profile of v0, /device:TPU:0, one launch (start us, length us, event | category | flops | bytes accessed | tf_op | source)
XLA Modules:
  0.0 35.4 jit_solution(5321207030614167832)
XLA Ops:
  0.6 0.0 copy-start
  0.7 0.7 %copy-done = s32[512]{0:T(512)S(1)} copy-done((s32[512]{0:T(512)S(1)}, s32[512]{0:T(512)}, u32[]{:S(2)}) %copy-start) | copy-done | bytes 2072
  1.3 0.6 %dynamic-slice_bitcast_fusion.limits_ref = s32[1,16]{1,0:T(1,128)} fusion(s32[512]{0:T(512)S(1)} %copy-done, s32[]{:T(128)S(6)} %select_n.3), kind=kLoop, calls=%fused_computation.1 | loop fusion | bytes 132 | tf_op jit(solution)/shard_map/broadcast_in_dim | solution.py:233
  1.9 1.5 %convert_bitcast_fusion.codes_ref = bf16[16,1024]{1,0:T(8,128)(2,1)} fusion(s32[1024,16]{0,1:T(8,128)} %param.3), kind=kLoop, calls=%fused_computation | loop fusion | flops 16384 | bytes 98304 | tf_op jit(solution)/shard_map/convert_element_type | solution.py:230
  3.4 2.0 %copy.5 = bf16[2,2,16,16,256]{4,2,0,1,3:T(8,128)(2,1)} copy(bf16[2,2,16,16,256]{4,3,2,1,0:T(8,128)(2,1)} %bitcast.10) | data formatting | bytes 1048576 | tf_op jit(solution)/shard_map/reshape | solution.py:231
  5.4 28.2 %retrieve.1 = (s32[16,128]{1,0:T(8,128)}, s32[1,16]{1,0:T(1,128)}) custom-call(bf16[16,1024]{1,0:T(8,128)(2,1)} %convert_bitcast_fusion.codes_ref, bf16[16,64,256]{2,1,0:T(8,128)(2,1)} %bitcast.9, s32[1,16]{1,0:T(1,128)} %dynamic-slice_bitcast_fusion.limits_ref), custom_call_target="tpu_custom_call" | custom-call | tf_op jit(solution)/shard_map/retrieve/pallas_call | solution.py:235
  33.5 0.0 copy-start.1
  33.6 1.3 %copy.8 = s32[16,128]{1,0:T(8,128)} copy(s32[16,128]{1,0:T(8,128)} %get-tuple-element.8) | data formatting | bytes 16384
  34.9 0.0 copy-done.1
  34.9 0.5 %copy.9 = s32[16]{0:T(128)} copy(s32[16]{0:T(128)S(1)} %bitcast.11) | data formatting | bytes 128
Async XLA Ops:
  0.6 0.7 %copy-start = (s32[512]{0:T(512)S(1)}, s32[512]{0:T(512)}, u32[]{:S(2)}) copy-start(s32[512]{0:T(512)} %param.5) | copy-start | bytes 6148
  33.5 1.3 %copy-start.1 = (s32[1,16]{1,0:T(1,128)S(1)}, s32[1,16]{1,0:T(1,128)}, u32[]{:S(2)}) copy-start(s32[1,16]{1,0:T(1,128)} %get-tuple-element.5) | copy-start | bytes 196
where the time goes:
time: 35.7 us; the launch traced here: 35.4 us
  Pallas kernels  28.2 us (79%)
  local copies, waits for them, and re-layouts  5.06 us (14%)
  other arithmetic  1.46 us (4%)
  between operations  0.66 us (2%)
    pallas_call x1, Pallas kernels, per_device(): pl.pallas_call(functools.partial(kernel, groups), out_shape=(jax.ShapeDty...  28.2 us
    unnamed x6, local copies, waits for them, and re-layouts  2.49 us
    reshape x1, local copies, waits for them, and re-layouts, per_device(): ordered = tables.reshape(2, 2, mine, width, K).transpose(3, 1, 0, 2, 4)  1.99 us
    convert_element_type x1, other arithmetic, per_device(): codes_t = codes.T.astype(jnp.bfloat16)  1.46 us

commit v1 on v0

--- a/solution.py
+++ b/solution.py
@@ -10,6 +10,7 @@
 K = 256
 SLOTS = 128
 LANES = 128
+F8 = jnp.float8_e4m3fn
 COLS = 256
 MESH = pl.DeviceIdType.MESH
 
@@ -25,12 +26,17 @@
 
 def kernel(
     groups,
-    codes_ref,
-    tables_ref,
-    limits_ref,
+    parts,
+    codes_hbm,
+    tables_hbm,
+    limits_hbm,
     ids_ref,
     count_ref,
+    codes_raw,
+    tables_raw,
+    limits_raw,
     codes_all,
+    tables_ref,
     part,
     recv1,
     send2,
@@ -38,6 +44,7 @@
     running,
     total,
     chosen,
+    load_sem,
     code_send,
     code_recv,
     send1_sem,
@@ -51,21 +58,30 @@
     high = sub // 2
     near = sub + 1 - 2 * low
     far = sub + 2 - 4 * high
-    width, rows = codes_ref.shape
+    width, rows = codes_raw.shape
     mine = ids_ref.shape[0]
+    half = groups // 2
+    partner = flip(db, 1, groups)
 
     barrier = pltpu.get_barrier_semaphore()
-    for step in range(1, groups):
+    pl.semaphore_signal(barrier, inc=1, device_id={"sub": far}, device_id_type=MESH)
+    for step in range(1, half):
         pl.semaphore_signal(
-            barrier, inc=1, device_id={"db": flip(db, step, groups)}, device_id_type=MESH
-        )
+            barrier, inc=1, device_id={"db": flip(db, 2 * step, groups)}, device_id_type=MESH
+        )
+    pl.semaphore_signal(barrier, inc=1, device_id={"db": partner}, device_id_type=MESH)
     pl.semaphore_signal(barrier, inc=1, device_id={"sub": near}, device_id_type=MESH)
-    pl.semaphore_signal(barrier, inc=1, device_id={"sub": far}, device_id_type=MESH)
-    pl.semaphore_wait(barrier, groups + 1)
+
+    load_codes = pltpu.make_async_copy(codes_hbm, codes_raw, load_sem.at[0])
+    load_tables = pltpu.make_async_copy(tables_hbm, tables_raw, load_sem.at[1])
+    load_limits = pltpu.make_async_copy(limits_hbm, limits_raw, load_sem.at[2])
+    load_codes.start()
+    load_tables.start()
+    load_limits.start()
 
     def code_copy(step):
         return pltpu.make_async_remote_copy(
-            src_ref=codes_ref,
+            src_ref=codes_all.at[db],
             dst_ref=codes_all.at[db],
             send_sem=code_send.at[step],
             recv_sem=code_recv.at[step],
@@ -73,9 +89,20 @@
             device_id_type=MESH,
         )
 
+    def relay_copy(step):
+        source = flip(db, step, groups)
+        return pltpu.make_async_remote_copy(
+            src_ref=codes_all.at[source],
+            dst_ref=codes_all.at[source],
+            send_sem=code_send.at[step + 1],
+            recv_sem=code_recv.at[step + 1],
+            device_id={"db": partner},
+            device_id_type=MESH,
+        )
+
     def near_copy(source):
         return pltpu.make_async_remote_copy(
-            src_ref=part.at[source, 1 - low],
+            src_ref=part.at[source, :, 1 - low],
             dst_ref=recv1.at[source],
             send_sem=send1_sem.at[source],
             recv_sem=recv1_sem.at[source],
@@ -93,26 +120,41 @@
             device_id_type=MESH,
         )
 
-    for step in range(1, groups):
-        code_copy(step).start()
-    codes_all[db] = codes_ref[...]
+    load_codes.wait()
+    codes_all[db] = codes_raw[...].astype(jnp.float32).astype(jnp.bfloat16)
+    pl.semaphore_wait(barrier, half + 2)
+    for step in range(half - 1, 0, -1):
+        code_copy(2 * step).start()
+    code_copy(1).start()
+
+    load_tables.wait()
+    tables_ref[...] = jnp.swapaxes(tables_raw[...], 0, 1)
+    load_limits.wait()
 
     centroid = lax.broadcasted_iota(jnp.int32, (K, LANES), 0).astype(jnp.float32)
     centroid = centroid.astype(jnp.bfloat16).reshape(K // 16, 16, LANES)
     centroid = jnp.concatenate([centroid] * (COLS // LANES), axis=2)
 
+    def order(place):
+        return 2 * (place % half) + place // half
+
     def pass_on(step):
         source = flip(db, step, groups)
         near_copy(source).wait_recv()
-        send2[source] = part[source, low, 1 - high] + recv1[source, 1 - high]
+        send2[source] = part[source, 1 - high, low] + recv1[source, 1 - high]
         far_copy(source).start()
 
-    def score(step, carry):
+    def score(place, carry):
+        step = order(place)
         source = flip(db, step, groups)
 
-        @pl.when(step > 0)
+        @pl.when(place > 0)
         def _():
             code_copy(step).wait_recv()
+
+            @pl.when(place < half)
+            def _():
+                relay_copy(step).start()
 
         def tile(j, carry):
             start = pl.multiple_of(j * COLS, COLS)
@@ -120,10 +162,13 @@
             acc = None
             for m in range(width):
                 row = jnp.broadcast_to(local[m : m + 1, :], (16, COLS)).astype(jnp.bfloat16)
-                hot = jnp.where(
-                    centroid == row[None], jnp.bfloat16(1), jnp.bfloat16(0)
-                ).reshape(K, COLS)
-                term = jnp.dot(tables_ref[m], hot, preferred_element_type=jnp.float32)
+                hot = jnp.where((centroid == row[None]).reshape(K, COLS), F8(1), F8(0))
+                term = lax.dot_general(
+                    tables_ref[m],
+                    hot,
+                    (((1,), (0,)), ((), ())),
+                    preferred_element_type=jnp.float32,
+                )
                 acc = term if acc is None else acc + term
             part[source, :, :, :, pl.ds(start, COLS)] = acc.reshape(2, 2, mine, COLS)
             return carry
@@ -131,9 +176,9 @@
         lax.fori_loop(0, rows // COLS, tile, 0, unroll=True)
         near_copy(source).start()
 
-        @pl.when(step > 0)
+        @pl.when(place > 0)
         def _():
-            pass_on(step - 1)
+            pass_on(order(place - 1))
 
         return carry
 
@@ -143,8 +188,13 @@
     diagonal = lax.broadcasted_iota(jnp.int32, (mine, mine), 0) == lax.broadcasted_iota(
         jnp.int32, (mine, mine), 1
     )
-    limit_row = jnp.broadcast_to(limits_ref[...].astype(jnp.float32), (mine, mine))
-    limit = jnp.sum(jnp.where(diagonal, limit_row, 0.0), axis=1, keepdims=True)
+    queries = limits_raw.shape[1]
+    first = (db * parts + sub) * mine
+    here = lax.broadcasted_iota(jnp.int32, (mine, queries), 1) == (
+        first + lax.broadcasted_iota(jnp.int32, (mine, queries), 0)
+    )
+    limit_row = jnp.broadcast_to(limits_raw[...].astype(jnp.float32), (mine, queries))
+    limit = jnp.sum(jnp.where(here, limit_row, 0.0), axis=1, keepdims=True)
     limit = jnp.broadcast_to(limit, (mine, LANES))
     blocks = rows // LANES
     upper_row = lax.broadcasted_iota(jnp.int32, (LANES, 2 * LANES), 0)
@@ -152,13 +202,13 @@
     upper = jnp.where(upper_row <= upper_col, 1.0, 0.0).astype(jnp.bfloat16)
 
     def match(step, carry):
-        source = flip(db, step, groups)
+        source = flip(db, 2 * (step % half) + step // half, groups)
         far_copy(source).wait_recv()
         flags = []
         for b in range(blocks):
             cut = pl.ds(b * LANES, LANES)
             distance = (
-                part[source, low, high, :, cut]
+                part[source, high, low, :, cut]
                 + recv1[source, high, :, cut]
                 + recv2[source, :, cut]
             )
@@ -225,23 +275,21 @@
     rows, width = codes.shape
     queries = tables.shape[0]
     mine = queries // parts
-    db = lax.axis_index("db")
-    sub = lax.axis_index("sub")
-    codes_t = codes.T.astype(jnp.bfloat16)
-    ordered = tables.reshape(2, 2, mine, width, K).transpose(3, 1, 0, 2, 4)
-    ordered = ordered.reshape(width, queries, K)
-    limit = lax.dynamic_slice_in_dim(limits, (db * parts + sub) * mine, mine)[None, :]
     blocks = groups * rows // LANES
     ids, counts = pl.pallas_call(
-        functools.partial(kernel, groups),
+        functools.partial(kernel, groups, parts),
         out_shape=(
             jax.ShapeDtypeStruct((mine, SLOTS), jnp.int32),
             jax.ShapeDtypeStruct((1, mine), jnp.int32),
         ),
-        in_specs=[pl.BlockSpec(memory_space=pltpu.VMEM)] * 3,
+        in_specs=[pl.BlockSpec(memory_space=pl.ANY)] * 3,
         out_specs=[pl.BlockSpec(memory_space=pltpu.VMEM)] * 2,
         scratch_shapes=[
+            pltpu.VMEM((width, rows), jnp.int32),
+            pltpu.VMEM(tables.shape, jnp.bfloat16),
+            pltpu.VMEM((1, limits.shape[0]), jnp.int32),
             pltpu.VMEM((groups, width, rows), jnp.bfloat16),
+            pltpu.VMEM((width, queries, K), jnp.bfloat16),
             pltpu.VMEM((groups, 2, 2, mine, rows), jnp.float32),
             pltpu.VMEM((groups, 2, mine, rows), jnp.float32),
             pltpu.VMEM((groups, mine, rows), jnp.float32),
@@ -249,6 +297,7 @@
             pltpu.VMEM((blocks * mine, LANES), jnp.float32),
             pltpu.VMEM((blocks * mine, LANES), jnp.float32),
             pltpu.VMEM((blocks * mine, LANES), jnp.float32),
+            pltpu.SemaphoreType.DMA((3,)),
             pltpu.SemaphoreType.DMA((groups,)),
             pltpu.SemaphoreType.DMA((groups,)),
             pltpu.SemaphoreType.DMA((groups,)),
@@ -260,7 +309,7 @@
             collective_id=0, has_side_effects=True, vmem_limit_bytes=60 * 1024 * 1024
         ),
         name="retrieve",
-    )(codes_t, ordered, limit)
+    )(codes.T, tables, limits[None, :])
     return ids, counts[0]
 
 

time: 35.7 us -> 26.7 us (0.75)
  Pallas kernels: 28.2 us -> 24.1 us
  local copies, waits for them, and re-layouts: 5.06 us -> 1.81 us
  other arithmetic: 1.46 us -> 0 us
    pallas_call x1, Pallas kernels: 28.2 us -> 24.1 us  [per_device(): pl.pallas_call(functools.partial(kernel, groups, parts), out_shape=(jax.S...]
    reshape x1 -> x0, local copies, waits for them, and re-layouts: 1.99 us -> none  [per_device(): ordered = tables.reshape(2, 2, mine, width, K).transpose(3, 1, 0, 2, 4)]
    convert_element_type x1 -> x0, other arithmetic: 1.46 us -> none  [per_device(): codes_t = codes.T.astype(jnp.bfloat16)]
    unnamed x6 -> x4, local copies, waits for them, and re-layouts: 2.49 us -> 1.81 us
    broadcast_in_dim x1 -> x0, local copies, waits for them, and re-layouts: 0.58 us -> none  [per_device(): lax.dynamic_slice_in_dim(limits, (db * parts + sub) * mine, mine)[None, :]]
where the time goes in v1:
time: 26.7 us; the launch traced here: 26.6 us
  Pallas kernels  24.1 us (90%)
  local copies, waits for them, and re-layouts  1.81 us (7%)
  between operations  0.65 us (2%)
    pallas_call x1, Pallas kernels, per_device(): pl.pallas_call(functools.partial(kernel, groups, parts), out_shape=(jax.S...  24.1 us
    unnamed x4, local copies, waits for them, and re-layouts  1.81 us

profile of v1, /device:TPU:0, one launch (start us, length us, event | category | flops | bytes accessed | tf_op | source)
XLA Modules:
  0.0 26.6 jit_solution(13887566590976710786)
XLA Ops:
  0.6 24.1 %retrieve.1 = (s32[16,128]{1,0:T(8,128)}, s32[1,16]{1,0:T(1,128)}) custom-call(s32[16,1024]{1,0:T(8,128)} %bitcast.3, bf16[64,16,256]{2,1,0:T(8,128)(2,1)} %tables_hbm.1, s32[1,512]{1,0:T(1,128)} %bitcast.4), custom_call_target="tpu_custom_call" | custom-call | tf_op jit(solution)/shard_map/retrieve/pallas_call | solution.py:279
  24.7 0.0 copy-start
  24.7 1.3 %copy.7 = s32[16,128]{1,0:T(8,128)} copy(s32[16,128]{1,0:T(8,128)} %get-tuple-element.8) | data formatting | bytes 16384
  26.0 0.0 copy-done
  26.0 0.5 %copy.8 = s32[16]{0:T(128)} copy(s32[16]{0:T(128)S(1)} %bitcast.5) | data formatting | bytes 128
Async XLA Ops:
  24.7 1.3 %copy-start = (s32[1,16]{1,0:T(1,128)S(1)}, s32[1,16]{1,0:T(1,128)}, u32[]{:S(2)}) copy-start(s32[1,16]{1,0:T(1,128)} %get-tuple-element.5) | copy-start | bytes 196

commit v2 on v1

--- a/solution.py
+++ b/solution.py
@@ -11,6 +11,10 @@
 SLOTS = 128
 LANES = 128
 F8 = jnp.float8_e4m3fn
+UNIT = 2.0**-10
+BITS = 22
+TOP = 2.0 ** (BITS - 10) - UNIT
+PART = BITS - 12
 COLS = 256
 MESH = pl.DeviceIdType.MESH
 
@@ -60,6 +64,7 @@
     far = sub + 2 - 4 * high
     width, rows = codes_raw.shape
     mine = ids_ref.shape[0]
+    quarter = rows // 4
     half = groups // 2
     partner = flip(db, 1, groups)
 
@@ -141,12 +146,23 @@
     def pass_on(step):
         source = flip(db, step, groups)
         near_copy(source).wait_recv()
-        send2[source] = part[source, 1 - high, low] + recv1[source, 1 - high]
+        value = part[source, 1 - high, low] + recv1[source, 1 - high]
+        count = (jnp.minimum(value, TOP) * (1.0 / UNIT)).astype(jnp.int32)
+        last = count[:, 3 * quarter :]
+        for k in range(3):
+            piece = jnp.bitwise_and(lax.shift_right_logical(last, k * PART), (1 << PART) - 1)
+            send2[source, k] = jnp.bitwise_or(
+                count[:, k * quarter : (k + 1) * quarter], lax.shift_left(piece, BITS)
+            )
         far_copy(source).start()
 
     def score(place, carry):
         step = order(place)
         source = flip(db, step, groups)
+
+        @pl.when(place == 1)
+        def _():
+            pass_on(order(place - 1))
 
         @pl.when(place > 0)
         def _():
@@ -173,17 +189,20 @@
             part[source, :, :, :, pl.ds(start, COLS)] = acc.reshape(2, 2, mine, COLS)
             return carry
 
-        lax.fori_loop(0, rows // COLS, tile, 0, unroll=True)
+        tiles = rows // COLS
+        lax.fori_loop(0, tiles // 2, tile, 0, unroll=True)
+
+        @pl.when(place > 2)
+        def _():
+            pass_on(order(place - 2))
+
+        lax.fori_loop(tiles // 2, tiles, tile, 0, unroll=True)
         near_copy(source).start()
-
-        @pl.when(place > 0)
-        def _():
-            pass_on(order(place - 1))
-
         return carry
 
     lax.fori_loop(0, groups, score, 0)
-    pass_on(groups - 1)
+    pass_on(order(groups - 2))
+    pass_on(order(groups - 1))
 
     diagonal = lax.broadcasted_iota(jnp.int32, (mine, mine), 0) == lax.broadcasted_iota(
         jnp.int32, (mine, mine), 1
@@ -204,13 +223,19 @@
     def match(step, carry):
         source = flip(db, 2 * (step % half) + step // half, groups)
         far_copy(source).wait_recv()
+        words = [recv2[source, k] for k in range(3)]
+        sent = [jnp.bitwise_and(word, (1 << BITS) - 1) for word in words]
+        rest = [lax.shift_right_logical(word, BITS) for word in words]
+        for k in range(1, 3):
+            rest[0] = jnp.bitwise_or(rest[0], lax.shift_left(rest[k], k * PART))
+        sent.append(rest[0])
         flags = []
         for b in range(blocks):
             cut = pl.ds(b * LANES, LANES)
+            at = b * LANES % quarter
+            other = sent[b * LANES // quarter][:, at : at + LANES].astype(jnp.float32)
             distance = (
-                part[source, high, low, :, cut]
-                + recv1[source, high, :, cut]
-                + recv2[source, :, cut]
+                part[source, high, low, :, cut] + recv1[source, high, :, cut] + other * UNIT
             )
             flags.append(jnp.where(distance <= limit, 1.0, 0.0).astype(jnp.bfloat16))
         sums = jnp.dot(
@@ -270,12 +295,26 @@
     lax.fori_loop(0, groups, drain, 0)
 
 
+def emit(ids_in, count_in, ids_ref, count_ref, sem):
+    ids = pltpu.make_async_copy(ids_in, ids_ref, sem.at[0])
+    count = pltpu.make_async_copy(count_in, count_ref, sem.at[1])
+    ids.start()
+    count.start()
+    ids.wait()
+    count.wait()
+
+
 def per_device(groups, parts, codes, tables, limits):
     assert parts == 4 and groups & (groups - 1) == 0
     rows, width = codes.shape
     queries = tables.shape[0]
     mine = queries // parts
     blocks = groups * rows // LANES
+    assert 2 * width * 128 <= 2 ** (BITS - 10)
+    held = [
+        pltpu.with_memory_space_constraint(array, pltpu.HBM)
+        for array in (codes.T, tables, limits[None, :])
+    ]
     ids, counts = pl.pallas_call(
         functools.partial(kernel, groups, parts),
         out_shape=(
@@ -292,8 +331,8 @@
             pltpu.VMEM((width, queries, K), jnp.bfloat16),
             pltpu.VMEM((groups, 2, 2, mine, rows), jnp.float32),
             pltpu.VMEM((groups, 2, mine, rows), jnp.float32),
-            pltpu.VMEM((groups, mine, rows), jnp.float32),
-            pltpu.VMEM((groups, mine, rows), jnp.float32),
+            pltpu.VMEM((groups, 3, mine, rows // 4), jnp.int32),
+            pltpu.VMEM((groups, 3, mine, rows // 4), jnp.int32),
             pltpu.VMEM((blocks * mine, LANES), jnp.float32),
             pltpu.VMEM((blocks * mine, LANES), jnp.float32),
             pltpu.VMEM((blocks * mine, LANES), jnp.float32),
@@ -306,10 +345,23 @@
             pltpu.SemaphoreType.DMA((groups,)),
         ],
         compiler_params=pltpu.CompilerParams(
-            collective_id=0, has_side_effects=True, vmem_limit_bytes=60 * 1024 * 1024
+            collective_id=0, has_side_effects=True, vmem_limit_bytes=48 * 1024 * 1024
         ),
         name="retrieve",
-    )(codes.T, tables, limits[None, :])
+    )(*held)
+
+    ids, counts = pl.pallas_call(
+        emit,
+        out_shape=(
+            jax.ShapeDtypeStruct((mine, SLOTS), jnp.int32),
+            jax.ShapeDtypeStruct((1, mine), jnp.int32),
+        ),
+        in_specs=[pl.BlockSpec(memory_space=pl.ANY)] * 2,
+        out_specs=[pl.BlockSpec(memory_space=pltpu.HBM)] * 2,
+        scratch_shapes=[pltpu.SemaphoreType.DMA((2,))],
+        compiler_params=pltpu.CompilerParams(vmem_limit_bytes=1024 * 1024),
+        name="emit",
+    )(ids, counts)
     return ids, counts[0]
 
 

time: 26.7 us -> 23.2 us (0.87)
  local copies, waits for them, and re-layouts: 1.81 us -> 0 us
  Pallas kernels: 24.1 us -> 22.5 us
    pallas_call x1, Pallas kernels: 24.1 us -> 21.8 us  [per_device(): pl.pallas_call(functools.partial(kernel, groups, parts), out_shape=(jax.S...]
    unnamed x4 -> x0, local copies, waits for them, and re-layouts: 1.81 us -> none
    pallas_call x0 -> x1, Pallas kernels: none -> 0.62 us  [per_device(): pl.pallas_call(emit, out_shape=(jax.ShapeDtypeStruct((mine, SLOTS), jnp.i...]
where the time goes in v2:
time: 23.2 us; the launch traced here: 23.1 us
  Pallas kernels  22.5 us (97%)
  between operations  0.64 us (3%)
    pallas_call x1, Pallas kernels, per_device(): pl.pallas_call(functools.partial(kernel, groups, parts), out_shape=(jax.S...  21.8 us
    pallas_call x1, Pallas kernels, per_device(): pl.pallas_call(emit, out_shape=(jax.ShapeDtypeStruct((mine, SLOTS), jnp.i...  0.62 us

profile of v2, /device:TPU:0, one launch (start us, length us, event | category | flops | bytes accessed | tf_op | source)
XLA Modules:
  0.0 23.1 jit_solution(11807861552876666629)
XLA Ops:
  0.6 21.8 %retrieve.1 = (s32[16,128]{1,0:T(8,128)S(1)}, s32[1,16]{1,0:T(1,128)S(1)}) custom-call(s32[16,1024]{1,0:T(8,128)} %bitcast.3, bf16[64,16,256]{2,1,0:T(8,128)(2,1)} %tables_hbm.1, s32[1,512]{1,0:T(1,128)} %bitcast.4), custom_call_target="tpu_custom_call" | custom-call | tf_op jit(solution)/shard_map/retrieve/pallas_call | solution.py:318
  22.5 0.6 %emit.1 = (s32[16,128]{1,0:T(8,128)}, s32[1,16]{1,0:T(1,128)}) custom-call(s32[16,128]{1,0:T(8,128)S(1)} %get-tuple-element.6.ids_in, s32[1,16]{1,0:T(1,128)S(1)} %get-tuple-element.7.count_in), custom_call_target="tpu_custom_call" | custom-call | tf_op jit(solution)/shard_map/emit/pallas_call | solution.py:353

commit v3 on v2

--- a/solution.py
+++ b/solution.py
@@ -16,6 +16,7 @@
 TOP = 2.0 ** (BITS - 10) - UNIT
 PART = BITS - 12
 COLS = 256
+BATCH = 2
 MESH = pl.DeviceIdType.MESH
 
 
@@ -189,19 +190,16 @@
             part[source, :, :, :, pl.ds(start, COLS)] = acc.reshape(2, 2, mine, COLS)
             return carry
 
-        tiles = rows // COLS
-        lax.fori_loop(0, tiles // 2, tile, 0, unroll=True)
-
-        @pl.when(place > 2)
+        lax.fori_loop(0, rows // COLS, tile, 0, unroll=True)
+        near_copy(source).start()
+
+        @pl.when(place > 1)
         def _():
-            pass_on(order(place - 2))
-
-        lax.fori_loop(tiles // 2, tiles, tile, 0, unroll=True)
-        near_copy(source).start()
+            pass_on(order(place - 1))
+
         return carry
 
     lax.fori_loop(0, groups, score, 0)
-    pass_on(order(groups - 2))
     pass_on(order(groups - 1))
 
     diagonal = lax.broadcasted_iota(jnp.int32, (mine, mine), 0) == lax.broadcasted_iota(
@@ -220,33 +218,37 @@
     upper_col = lax.broadcasted_iota(jnp.int32, (LANES, 2 * LANES), 1)
     upper = jnp.where(upper_row <= upper_col, 1.0, 0.0).astype(jnp.bfloat16)
 
-    def match(step, carry):
-        source = flip(db, 2 * (step % half) + step // half, groups)
-        far_copy(source).wait_recv()
-        words = [recv2[source, k] for k in range(3)]
-        sent = [jnp.bitwise_and(word, (1 << BITS) - 1) for word in words]
-        rest = [lax.shift_right_logical(word, BITS) for word in words]
-        for k in range(1, 3):
-            rest[0] = jnp.bitwise_or(rest[0], lax.shift_left(rest[k], k * PART))
-        sent.append(rest[0])
+    def match(turn, carry):
         flags = []
-        for b in range(blocks):
-            cut = pl.ds(b * LANES, LANES)
-            at = b * LANES % quarter
-            other = sent[b * LANES // quarter][:, at : at + LANES].astype(jnp.float32)
-            distance = (
-                part[source, high, low, :, cut] + recv1[source, high, :, cut] + other * UNIT
-            )
-            flags.append(jnp.where(distance <= limit, 1.0, 0.0).astype(jnp.bfloat16))
+        for k in range(BATCH):
+            source = flip(db, order(turn * BATCH + k), groups)
+            far_copy(source).wait_recv()
+            words = [recv2[source, k] for k in range(3)]
+            sent = [jnp.bitwise_and(word, (1 << BITS) - 1) for word in words]
+            rest = [lax.shift_right_logical(word, BITS) for word in words]
+            for k in range(1, 3):
+                rest[0] = jnp.bitwise_or(rest[0], lax.shift_left(rest[k], k * PART))
+            sent.append(rest[0])
+            for b in range(blocks):
+                cut = pl.ds(b * LANES, LANES)
+                at = b * LANES % quarter
+                other = sent[b * LANES // quarter][:, at : at + LANES].astype(jnp.float32)
+                distance = (
+                    part[source, high, low, :, cut] + recv1[source, high, :, cut] + other * UNIT
+                )
+                flags.append(jnp.where(distance <= limit, 1.0, 0.0).astype(jnp.bfloat16))
         sums = jnp.dot(
             jnp.concatenate(flags, axis=0), upper, preferred_element_type=jnp.float32
         )
-        here = pl.ds(pl.multiple_of(source * (blocks * mine), blocks * mine), blocks * mine)
-        running[here, :] = sums[:, :LANES]
-        total[here, :] = sums[:, LANES:]
+        size = blocks * mine
+        for k in range(BATCH):
+            source = flip(db, order(turn * BATCH + k), groups)
+            here = pl.ds(pl.multiple_of(source * size, size), size)
+            running[here, :] = sums[k * size : (k + 1) * size, :LANES]
+            total[here, :] = sums[k * size : (k + 1) * size, LANES:]
         return carry
 
-    lax.fori_loop(0, groups, match, 0)
+    lax.fori_loop(0, groups // BATCH, match, 0)
 
     slot = lax.broadcasted_iota(jnp.int32, (mine, SLOTS), 1).astype(jnp.float32)
 

time: 23.2 us -> 22.8 us (0.983)
  Pallas kernels: 22.5 us -> 22 us
    pallas_call x1, Pallas kernels: 21.8 us -> 21.4 us  [per_device(): pl.pallas_call(functools.partial(kernel, groups, parts), out_shape=(jax.S...]
where the time goes in v3:
time: 22.8 us; the launch traced here: 22.6 us
  Pallas kernels  22 us (96%)
  between operations  0.64 us (3%)
    pallas_call x1, Pallas kernels, per_device(): pl.pallas_call(functools.partial(kernel, groups, parts), out_shape=(jax.S...  21.4 us
    pallas_call x1, Pallas kernels, per_device(): pl.pallas_call(emit, out_shape=(jax.ShapeDtypeStruct((mine, SLOTS), jnp.i...  0.62 us

profile of v3, /device:TPU:0, one launch (start us, length us, event | category | flops | bytes accessed | tf_op | source)
XLA Modules:
  0.0 22.6 jit_solution(6687520150913261006)
XLA Ops:
  0.6 21.4 %retrieve.1 = (s32[16,128]{1,0:T(8,128)S(1)}, s32[1,16]{1,0:T(1,128)S(1)}) custom-call(s32[16,1024]{1,0:T(8,128)} %bitcast.3, bf16[64,16,256]{2,1,0:T(8,128)(2,1)} %tables_hbm.1, s32[1,512]{1,0:T(1,128)} %bitcast.4), custom_call_target="tpu_custom_call" | custom-call | tf_op jit(solution)/shard_map/retrieve/pallas_call | solution.py:320
  22.0 0.6 %emit.1 = (s32[16,128]{1,0:T(8,128)}, s32[1,16]{1,0:T(1,128)}) custom-call(s32[16,128]{1,0:T(8,128)S(1)} %get-tuple-element.6.ids_in, s32[1,16]{1,0:T(1,128)S(1)} %get-tuple-element.7.count_in), custom_call_target="tpu_custom_call" | custom-call | tf_op jit(solution)/shard_map/emit/pallas_call | solution.py:355

commit v4 on v3

--- a/solution.py
+++ b/solution.py
@@ -129,9 +129,9 @@
     load_codes.wait()
     codes_all[db] = codes_raw[...].astype(jnp.float32).astype(jnp.bfloat16)
     pl.semaphore_wait(barrier, half + 2)
-    for step in range(half - 1, 0, -1):
+    code_copy(1).start()
+    for step in range(1, half):
         code_copy(2 * step).start()
-    code_copy(1).start()
 
     load_tables.wait()
     tables_ref[...] = jnp.swapaxes(tables_raw[...], 0, 1)

time: 22.8 us -> 22.5 us (0.987)
  Pallas kernels: 22 us -> 21.7 us
    pallas_call x1, Pallas kernels: 21.4 us -> 21.1 us  [per_device(): pl.pallas_call(functools.partial(kernel, groups, parts), out_shape=(jax.S...]
where the time goes in v4:
time: 22.5 us; the launch traced here: 22.4 us
  Pallas kernels  21.7 us (96%)
  between operations  0.64 us (3%)
    pallas_call x1, Pallas kernels, per_device(): pl.pallas_call(functools.partial(kernel, groups, parts), out_shape=(jax.S...  21.1 us
    pallas_call x1, Pallas kernels, per_device(): pl.pallas_call(emit, out_shape=(jax.ShapeDtypeStruct((mine, SLOTS), jnp.i...  0.62 us

profile of v4, /device:TPU:0, one launch (start us, length us, event | category | flops | bytes accessed | tf_op | source)
XLA Modules:
  0.0 22.4 jit_solution(15659930811528468494)
XLA Ops:
  0.6 21.1 %retrieve.1 = (s32[16,128]{1,0:T(8,128)S(1)}, s32[1,16]{1,0:T(1,128)S(1)}) custom-call(s32[16,1024]{1,0:T(8,128)} %bitcast.3, bf16[64,16,256]{2,1,0:T(8,128)(2,1)} %tables_hbm.1, s32[1,512]{1,0:T(1,128)} %bitcast.4), custom_call_target="tpu_custom_call" | custom-call | tf_op jit(solution)/shard_map/retrieve/pallas_call | solution.py:320
  21.8 0.6 %emit.1 = (s32[16,128]{1,0:T(8,128)}, s32[1,16]{1,0:T(1,128)}) custom-call(s32[16,128]{1,0:T(8,128)S(1)} %get-tuple-element.6.ids_in, s32[1,16]{1,0:T(1,128)S(1)} %get-tuple-element.7.count_in), custom_call_target="tpu_custom_call" | custom-call | tf_op jit(solution)/shard_map/emit/pallas_call | solution.py:355
